TPU v7x, 256 devices: a whole 4x4x8 slice. The times are simulated.
256 devices in a mesh: batch: 64 (over z, y, core), group: 4 (over x).
Axes of the slice: x: 4, y: 4, z: 8, core: 2. Of those that a mesh axis runs over, the one named last changes fastest.
Arguments:
- samples_in: float32 [16384, 8192], P('batch', 'group'), may hold values from -8 to 8, as said below
- second_samples_in: float32 [16384, 8192], P('batch', 'group'), may hold values from -8 to 8, as said below
Outputs:
- standard: float32 [16384, 8192], P(None, ('group', 'batch'))
- second_standard: float32 [16384, 8192], P(None, ('group', 'batch'))
Inputs may be any that keep to these rules, and one draw needn't show every extreme that they name: samples_in holds numbers from -8 to 8. second_samples_in holds numbers from -8 to 8.
All inputs are finite; a program needn't handle non-finite values.
Results may differ from a plain program's by a relative error of at most 0.0003.
Values sent between devices are 32-bit elements.
A program may use at most 64 MiB of HBM per device.

v0:
```python
import jax
import jax.numpy as jnp
from jax import lax
from jax.sharding import PartitionSpec as P


def shards(samples_in, second_samples_in):
    moved_samples_in, moved_second_samples_in = (
        lax.all_to_all(samples_in, "batch", split_axis=1, concat_axis=0, tiled=True),
        lax.all_to_all(second_samples_in, "batch", split_axis=1, concat_axis=0, tiled=True),
    )
    wide_standard = moved_samples_in.astype(jnp.float32)
    low_standard = jnp.mean(jnp.minimum(wide_standard, 1.0), axis=0)
    high_standard = jnp.mean(jnp.maximum(wide_standard, 1.0), axis=0)
    standard = (wide_standard - low_standard) / (high_standard - low_standard + 0.1)
    wide_second_standard = moved_second_samples_in.astype(jnp.float32)
    low_second_standard = jnp.mean(jnp.minimum(wide_second_standard, 1.0), axis=0)
    high_second_standard = jnp.mean(jnp.maximum(wide_second_standard, 1.0), axis=0)
    second_standard = (wide_second_standard - low_second_standard) / (
        high_second_standard - low_second_standard + 0.1
    )
    return (standard, second_standard)


def solution(mesh):
    placed = (P("batch", "group"), P("batch", "group"))
    return jax.shard_map(
        shards,
        mesh=mesh,
        in_specs=placed,
        out_specs=(P(None, ("group", "batch")), P(None, ("group", "batch"))),
        check_vma=False,
    )
```

profile of v0, /device:TPU:1, one launch (start us, length us, event | category | flops | bytes accessed | tf_op | source)
XLA Modules:
  0.0 131.2 jit_solution(1212408912967715892)
XLA Ops:
  0.6 2.9 %copy.8 = f32[256,2048]{0,1:T(8,128)} copy(f32[256,2048]{1,0:T(8,128)} %param.2) | data formatting | bytes 4194304 | tf_op args[0]
  3.5 13.2 %all-to-all-start = ((f32[256,64,32]{0,2,1:T(8,128)}), f32[256,64,32]{0,2,1:T(8,128)S(1)}, u32[]{:S(2)}, u32[]{:S(2)}) async-start(f32[256,64,32]{0,2,1:T(8,128)} %bitcast.24), calls=%async_computation | async-start | bytes 4194304 | tf_op jit(solution)/shard_map/all_to_all | solution.py:9
  16.7 2.9 %copy.10 = f32[256,2048]{0,1:T(8,128)} copy(f32[256,2048]{1,0:T(8,128)} %param.3) | data formatting | bytes 4194304 | tf_op args[1]
  19.6 47.1 %all-to-all-done = f32[256,64,32]{0,2,1:T(8,128)S(1)} async-done(((f32[256,64,32]{0,2,1:T(8,128)}), f32[256,64,32]{0,2,1:T(8,128)S(1)}, u32[]{:S(2)}, u32[]{:S(2)}) %all-to-all-start) | async-done | bytes 2097184 | tf_op jit(solution)/shard_map/all_to_all | solution.py:9
  66.6 7.4 %all-to-all-start.1 = ((f32[256,64,32]{0,2,1:T(8,128)}), f32[256,64,32]{0,2,1:T(8,128)}, u32[]{:S(2)}, u32[]{:S(2)}) async-start(f32[256,64,32]{0,2,1:T(8,128)} %bitcast.23), calls=%async_computation.1 | async-start | bytes 4194304 | tf_op jit(solution)/shard_map/all_to_all | solution.py:10
  74.1 1.5 %copy.12 = f32[64,4,8,256]{3,2,0,1:T(8,128)} copy(f32[64,4,8,256]{3,2,1,0:T(8,128)S(1)} %bitcast.20) | data formatting | bytes 4194304 | tf_op jit(solution)/shard_map/all_to_all | solution.py:9
  75.6 48.7 %all-to-all-done.1 = f32[256,64,32]{0,2,1:T(8,128)} async-done(((f32[256,64,32]{0,2,1:T(8,128)}), f32[256,64,32]{0,2,1:T(8,128)}, u32[]{:S(2)}, u32[]{:S(2)}) %all-to-all-start.1) | async-done | bytes 2097184 | tf_op jit(solution)/shard_map/all_to_all | solution.py:10
  124.2 1.8 %copy.13 = f32[64,4,8,256]{3,2,0,1:T(8,128)S(1)} copy(f32[64,4,8,256]{3,2,1,0:T(8,128)} %bitcast.6) | data formatting | bytes 4194304 | tf_op jit(solution)/shard_map/all_to_all | solution.py:10
  126.0 0.0 copy-start
  126.0 0.5 fusion.3
  126.5 2.1 %fusion.1 = (f32[32]{0:T(128)S(1)}, f32[32]{0:T(128)S(1)}) fusion(f32[256,64,32]{0,2,1:T(8,128)} %all-to-all-done.1), kind=kLoop, calls=%fused_computation.3 | loop fusion | flops 2097088 | bytes 2097408 | tf_op jit(solution)/shard_map/reduce_sum | solution.py:17
  128.7 0.0 copy-done
  128.7 2.5 %subtract_divide_fusion = (f32[16384,32]{0,1:T(8,128)}, f32[16384,32]{0,1:T(8,128)}) fusion(f32[16384,32]{0,1:T(8,128)S(1)} %bitcast.22, f32[32]{0:T(128)S(1)} %get-tuple-element.7, f32[32]{0:T(128)S(1)} %get-tuple-element.6, f32[32]{0:T(128)S(1)} %get-tuple-element.9, f32[16384,32]{0,1:T(8,128)S(1)} %bitcast.21, f32[32]{0:T(128)S(1)} %get-tuple-element.8), kind=kLoop, calls=%fused_computation.8 | loop fusion | flops 2097152 | bytes 8389120 | tf_op jit(solution)/shard_map/div | solution.py:19
  (2 shorter events, 0.0 us)
Async XLA Ops:
  3.5 63.1 %all-to-all-start = ((f32[256,64,32]{0,2,1:T(8,128)}), f32[256,64,32]{0,2,1:T(8,128)S(1)}, u32[]{:S(2)}, u32[]{:S(2)}) async-start(f32[256,64,32]{0,2,1:T(8,128)} %bitcast.24), calls=%async_computation | async-start | bytes 4194304 | tf_op jit(solution)/shard_map/all_to_all | solution.py:9
  66.6 57.6 %all-to-all-start.1 = ((f32[256,64,32]{0,2,1:T(8,128)}), f32[256,64,32]{0,2,1:T(8,128)}, u32[]{:S(2)}, u32[]{:S(2)}) async-start(f32[256,64,32]{0,2,1:T(8,128)} %bitcast.23), calls=%async_computation.1 | async-start | bytes 4194304 | tf_op jit(solution)/shard_map/all_to_all | solution.py:10
  126.0 2.6 %copy-start = (f32[64,4,8,256]{3,2,0,1:T(8,128)S(1)}, f32[64,4,8,256]{3,2,0,1:T(8,128)}, u32[]{:S(2)}) copy-start(f32[64,4,8,256]{3,2,0,1:T(8,128)} %copy.12) | copy-start | bytes 6291460
where the time goes:
time: 132 us; the launch traced here: 131 us
  waiting for transfers between devices  95.7 us (72%)
  starting transfers between devices  20.6 us (16%)
  local copies, waits for them, and re-layouts  9.08 us (7%)
  other arithmetic  5.11 us (4%)
    all_to_all x1, waiting for transfers between devices, shards(): lax.all_to_all(second_samples_in, 'batch', split_axis=1, concat_axis=0, t...  48.7 us
    all_to_all x1, waiting for transfers between devices, shards(): lax.all_to_all(samples_in, 'batch', split_axis=1, concat_axis=0, tiled=True)  47.1 us
    all_to_all x1, starting transfers between devices, shards(): lax.all_to_all(samples_in, 'batch', split_axis=1, concat_axis=0, tiled=True)  13.2 us
    all_to_all x1, starting transfers between devices, shards(): lax.all_to_all(second_samples_in, 'batch', split_axis=1, concat_axis=0, t...  7.41 us
    unnamed x4, local copies, waits for them, and re-layouts  5.78 us
  transfers between devices with their start and end apart: 2, of which 2 were waited for; matrix products, arithmetic and copies ran while one was open for 3% of the time, Pallas kernels for 0%

commit v1 on v0

v1 whole, which is shorter than its diff:
```python
import functools

import jax
import jax.numpy as jnp
from jax import lax
from jax.experimental import pallas as pl
from jax.experimental.pallas import tpu as pltpu
from jax.sharding import PartitionSpec as P

MESH = pl.DeviceIdType.MESH
NZ, NY, NC = 8, 4, 2
PLANE = NY * NC
PEERS = NZ * PLANE
HOPS = (1, 7, 2, 6, 3, 5, 4, 0)


def move_kernel(
    a_ref, b_ref, ra_ref, rb_ref, stats_ref, held, blocks, load_sems, send_sems, recv_sems
):
    rows = a_ref.shape[0]
    width = a_ref.shape[1] // PEERS
    span = width * PLANE
    total = rows * PEERS
    me = lax.axis_index("batch")
    group = lax.axis_index("group")
    z, y, c = me // PLANE, lax.rem(me // NC, NY), lax.rem(me, NC)
    sources, landed = (a_ref, b_ref), (ra_ref, rb_ref)

    barrier = pltpu.get_barrier_semaphore()

    def greet(k, carry):
        pl.semaphore_signal(
            barrier, inc=1, device_id=(lax.rem(me + k, PEERS), group), device_id_type=MESH
        )
        return carry

    def load(i, hop):
        plane = lax.rem(z + hop, NZ)
        columns = pl.ds(pl.multiple_of(plane * span, span), span)
        return pltpu.make_async_copy(
            sources[i].at[:, columns], held.at[i, :, columns], load_sems.at[i, hop]
        )

    def turn(i, hop):
        load(i, hop).wait()
        plane = lax.rem(z + hop, NZ)
        for part in range(span // 128):
            columns = pl.ds(pl.multiple_of(plane * span + part * 128, 128), 128)
            tile = held[i, :, columns].T
            per = 128 // width
            first = plane * PLANE + part * per
            for k in range(per):
                blocks[i, first + k] = tile[k * width : (k + 1) * width]

    def send(i, hop):
        plane = lax.rem(z + hop, NZ)
        for dy in range(NY):
            for dc in range(NC):
                if (hop, dy, dc) == (0, 0, 0):
                    continue
                to = plane * PLANE + lax.rem(y + dy, NY) * NC + lax.rem(c + dc, NC)
                pltpu.make_async_remote_copy(
                    src_ref=blocks.at[i, to],
                    dst_ref=landed[i].at[me],
                    send_sem=send_sems.at[i],
                    recv_sem=recv_sems.at[i, hop],
                    device_id=(to, group),
                    device_id_type=MESH,
                ).start()

    def gather(i, hop, sums):
        plane = lax.rem(z - hop + NZ, NZ)
        count = PLANE - 1 if hop == 0 else PLANE
        whole = landed[i].at[pl.ds(0, count)]
        pltpu.make_async_copy(whole, whole, recv_sems.at[i, hop]).wait()
        low, high = sums
        for k in range(PLANE):
            for part in range(rows // 128):
                x = landed[i][plane * PLANE + k, :, part * 128 : (part + 1) * 128]
                low += jnp.minimum(x, 1.0)
                high += jnp.maximum(x, 1.0)
        return low, high

    lax.fori_loop(1, PEERS, greet, 0)
    for i in range(2):
        for hop in HOPS:
            load(i, hop).start()
    for hop in HOPS:
        turn(0, hop)
    ra_ref[me] = blocks[0, me]
    pl.semaphore_wait(barrier, PEERS - 1)
    for hop in HOPS:
        send(0, hop)
    for hop in HOPS:
        turn(1, hop)
    rb_ref[me] = blocks[1, me]
    for hop in HOPS:
        send(1, hop)
    for i in range(2):
        zero = jnp.zeros((width, 128), jnp.float32)
        sums = (zero, zero)
        for hop in HOPS:
            sums = gather(i, hop, sums)
        low = jnp.sum(sums[0], axis=1, keepdims=True) * (1.0 / total)
        high = jnp.sum(sums[1], axis=1, keepdims=True) * (1.0 / total)
        stats_ref[2 * i] = jnp.broadcast_to(low, (width, 128))
        stats_ref[2 * i + 1] = jnp.broadcast_to(1.0 / (high - low + 0.1), (width, 128))
    for i in range(2):
        whole = blocks.at[i, pl.ds(0, PEERS - 1)]
        pltpu.make_async_copy(whole, whole, send_sems.at[i]).wait()


def scale_kernel(ra_ref, rb_ref, stats_ref, oa_ref, ob_ref, ready, sems):
    peers, width, rows = ra_ref.shape
    pieces = 8
    per = peers // pieces
    copies = []
    for i, (landed, out) in enumerate(((ra_ref, oa_ref), (rb_ref, ob_ref))):
        low, scale = stats_ref[2 * i], stats_ref[2 * i + 1]
        for piece in range(pieces):
            for k in range(piece * per, (piece + 1) * per):
                for part in range(0, rows, 128):
                    x = landed[k, :, part : part + 128]
                    ready[i, :, k * rows + part : k * rows + part + 128] = (x - low) * scale
            columns = pl.ds(piece * per * rows, per * rows)
            copy = pltpu.make_async_copy(
                ready.at[i, :, columns], out.at[:, columns], sems.at[i, piece]
            )
            copy.start()
            copies.append(copy)
    for copy in copies:
        copy.wait()


def shards(a, b):
    rows, width = a.shape[0], a.shape[1] // PEERS
    block = (PEERS, width, rows)
    ra, rb, stats = pl.pallas_call(
        move_kernel,
        out_shape=(
            pltpu.VMEM(block, jnp.float32),
            pltpu.VMEM(block, jnp.float32),
            pltpu.VMEM((4, width, 128), jnp.float32),
        ),
        in_specs=[pl.BlockSpec(memory_space=pltpu.HBM)] * 2,
        out_specs=[pl.BlockSpec(memory_space=pltpu.VMEM)] * 3,
        scratch_shapes=[
            pltpu.VMEM((2,) + a.shape, jnp.float32),
            pltpu.VMEM((2,) + block, jnp.float32),
            pltpu.SemaphoreType.DMA((2, NZ)),
            pltpu.SemaphoreType.DMA((2,)),
            pltpu.SemaphoreType.DMA((2, NZ)),
        ],
        compiler_params=pltpu.CompilerParams(
            collective_id=0, has_side_effects=True, vmem_limit_bytes=58 << 20
        ),
        name="move",
    )(a, b)
    wide = jax.ShapeDtypeStruct((width, PEERS * rows), jnp.float32)
    oa, ob = pl.pallas_call(
        scale_kernel,
        out_shape=(wide, wide),
        in_specs=[pl.BlockSpec(memory_space=pltpu.VMEM)] * 3,
        out_specs=[pl.BlockSpec(memory_space=pltpu.HBM)] * 2,
        scratch_shapes=[
            pltpu.VMEM((2,) + wide.shape, jnp.float32),
            pltpu.SemaphoreType.DMA((2, 8)),
        ],
        compiler_params=pltpu.CompilerParams(vmem_limit_bytes=24 << 20),
        name="scale",
    )(ra, rb, stats)
    return oa.T, ob.T


def solution(mesh):
    placed = (P("batch", "group"), P("batch", "group"))
    return jax.shard_map(
        shards,
        mesh=mesh,
        in_specs=placed,
        out_specs=(P(None, ("group", "batch")), P(None, ("group", "batch"))),
        check_vma=False,
    )
```

time: 132 us -> 109 us (0.83)
  Pallas kernels: 0 us -> 108 us
  waiting for transfers between devices: 95.7 us -> 0 us
  starting transfers between devices: 20.6 us -> 0 us
  local copies, waits for them, and re-layouts: 9.08 us -> 0 us
  other arithmetic: 5.11 us -> 0 us
    pallas_call x0 -> x2, Pallas kernels: none -> 108 us  [the longest x1 106 us: shards(): pl.pallas_call(move_kernel, out_shape=(pltpu.VMEM(block, jnp.float32), pl...]
    all_to_all x2 -> x0, waiting for transfers between devices: 95.7 us -> none  [the longest x1 48.7 us: shards(): lax.all_to_all(second_samples_in, 'batch', split_axis=1, concat_axis=0, t...]
    all_to_all x2 -> x0, starting transfers between devices: 20.6 us -> none  [the longest x1 13.2 us: shards(): lax.all_to_all(samples_in, 'batch', split_axis=1, concat_axis=0, tiled=True)]
    unnamed x4 -> x0, local copies, waits for them, and re-layouts: 5.78 us -> none
    all_to_all x2 -> x0, local copies, waits for them, and re-layouts: 3.3 us -> none  [the longest x1 1.78 us: shards(): lax.all_to_all(second_samples_in, 'batch', split_axis=1, concat_axis=0, t...]
    reduce_sum x2 -> x0, other arithmetic: 2.61 us -> none  [the longest x1 2.14 us: shards(): jnp.mean(jnp.minimum(wide_second_standard, 1.0), axis=0)]
    div x3 -> x0, other arithmetic: 2.51 us -> none  [the longest x1 2.49 us: shards(): (wide_second_standard - low_second_standard) / (high_second_standard - lo...]
  transfers between devices with their start and end apart: 2 -> 0, of which waited for: 2 -> 0; matrix products, arithmetic and copies ran while one was open for 3% -> 0% of each run, Pallas kernels for 0% -> 0%
where the time goes in v1:
time: 109 us
  Pallas kernels  108 us (99%)
    pallas_call x1, Pallas kernels, shards(): pl.pallas_call(move_kernel, out_shape=(pltpu.VMEM(block, jnp.float32), pl...  106 us

profile of v1, /device:TPU:1, one launch (start us, length us, event | category | flops | bytes accessed | tf_op | source)
XLA Modules:
  0.0 108.9 jit_solution(10652613829111647177)
XLA Ops:
  0.6 106.1 %move.1 = (f32[64,32,256]{2,1,0:T(8,128)S(1)}, f32[64,32,256]{2,1,0:T(8,128)S(1)}, f32[4,32,128]{2,1,0:T(8,128)S(1)}) custom-call(f32[256,2048]{1,0:T(8,128)} %a_ref.1, f32[256,2048]{1,0:T(8,128)} %b_ref.1), custom_call_target="tpu_custom_call" | custom-call | tf_op jit(solution)/shard_map/move/pallas_call | solution.py:138
  106.7 2.2 %scale.1 = (f32[32,16384]{1,0:T(8,128)}, f32[32,16384]{1,0:T(8,128)}) custom-call(f32[64,32,256]{2,1,0:T(8,128)S(1)} %get-tuple-element.7.ra_ref, f32[64,32,256]{2,1,0:T(8,128)S(1)} %get-tuple-element.8.rb_ref, f32[4,32,128]{2,1,0:T(8,128)S(1)} %get-tuple-element.9.stats_ref), custom_call_target="tpu_custom_call" | custom-call | tf_op jit(solution)/shard_map/scale/pallas_call | solution.py:160

commit v2 on v1

--- a/solution.py
+++ b/solution.py
@@ -12,10 +12,24 @@
 PLANE = NY * NC
 PEERS = NZ * PLANE
 HOPS = (1, 7, 2, 6, 3, 5, 4, 0)
+OFFSETS = tuple(
+    ((5 * k + 5) % NZ, (k // NZ * 3 + k) % NY, k // (NZ * NY)) for k in range(PEERS)
+)
+NEAR = tuple(
+    (hop, dy, dc)
+    for hop, dy, dc in OFFSETS
+    if (hop == 0 and dy + dc > 0) or (hop in (1, 7) and dy == 0)
+)
+FIRST = ((1, 0, 0), (7, 0, 0), (1, 0, 1), (7, 0, 1))
+SECOND = tuple((hop, dy, dc) for dy in (1, 2, 3) for dc in (0, 1) for hop in (1, 7))
+THIRD = tuple(o for o in OFFSETS if o[0] not in (1, 7, 4) and o != (0, 0, 0))
+LAST = tuple((0, o) for o in OFFSETS if o[0] == 4) + tuple(
+    (1, o) for o in OFFSETS if o != (0, 0, 0)
+)
 
 
 def move_kernel(
-    a_ref, b_ref, ra_ref, rb_ref, stats_ref, held, blocks, load_sems, send_sems, recv_sems
+    a_ref, b_ref, ra_ref, rb_ref, stats_ref, held, blocks, load_sems, send_sems, recv_sems, known
 ):
     rows = a_ref.shape[0]
     width = a_ref.shape[1] // PEERS
@@ -26,13 +40,13 @@
     z, y, c = me // PLANE, lax.rem(me // NC, NY), lax.rem(me, NC)
     sources, landed = (a_ref, b_ref), (ra_ref, rb_ref)
 
-    barrier = pltpu.get_barrier_semaphore()
-
-    def greet(k, carry):
+    def peer(hop, dy, dc):
+        return lax.rem(z + hop, NZ) * PLANE + lax.rem(y + dy, NY) * NC + lax.rem(c + dc, NC)
+
+    def signal(semaphore, *offset):
         pl.semaphore_signal(
-            barrier, inc=1, device_id=(lax.rem(me + k, PEERS), group), device_id_type=MESH
+            semaphore, inc=1, device_id=(peer(*offset), group), device_id_type=MESH
         )
-        return carry
 
     def load(i, hop):
         plane = lax.rem(z + hop, NZ)
@@ -52,21 +66,17 @@
             for k in range(per):
                 blocks[i, first + k] = tile[k * width : (k + 1) * width]
 
-    def send(i, hop):
-        plane = lax.rem(z + hop, NZ)
-        for dy in range(NY):
-            for dc in range(NC):
-                if (hop, dy, dc) == (0, 0, 0):
-                    continue
-                to = plane * PLANE + lax.rem(y + dy, NY) * NC + lax.rem(c + dc, NC)
-                pltpu.make_async_remote_copy(
-                    src_ref=blocks.at[i, to],
-                    dst_ref=landed[i].at[me],
-                    send_sem=send_sems.at[i],
-                    recv_sem=recv_sems.at[i, hop],
-                    device_id=(to, group),
-                    device_id_type=MESH,
-                ).start()
+    def send(i, offsets):
+        for hop, dy, dc in offsets:
+            to = peer(hop, dy, dc)
+            pltpu.make_async_remote_copy(
+                src_ref=blocks.at[i, to],
+                dst_ref=landed[i].at[me],
+                send_sem=send_sems.at[i],
+                recv_sem=recv_sems.at[i, hop],
+                device_id=(to, group),
+                device_id_type=MESH,
+            ).start()
 
     def gather(i, hop, sums):
         plane = lax.rem(z - hop + NZ, NZ)
@@ -81,21 +91,36 @@
                 high += jnp.maximum(x, 1.0)
         return low, high
 
-    lax.fori_loop(1, PEERS, greet, 0)
+    barrier = pltpu.get_barrier_semaphore()
+    for offset in NEAR:
+        signal(barrier, *offset)
     for i in range(2):
         for hop in HOPS:
             load(i, hop).start()
-    for hop in HOPS:
+    turn(0, 1)
+    turn(0, 7)
+    pl.semaphore_wait(barrier, len(NEAR))
+    signal(known.at[0], 1, 0, 0)
+    signal(known.at[0], 7, 0, 0)
+    send(0, FIRST)
+    turn(0, 2)
+    turn(0, 6)
+    pl.semaphore_wait(known.at[0], 2)
+    signal(known.at[1], 2, 0, 0)
+    signal(known.at[1], 6, 0, 0)
+    send(0, SECOND)
+    for hop in (3, 5, 4, 0):
         turn(0, hop)
-    ra_ref[me] = blocks[0, me]
-    pl.semaphore_wait(barrier, PEERS - 1)
-    for hop in HOPS:
-        send(0, hop)
+    pl.semaphore_wait(known.at[1], 2)
+    signal(known.at[2], 7, 0, 0)
+    send(0, THIRD)
     for hop in HOPS:
         turn(1, hop)
+    ra_ref[me] = blocks[0, me]
     rb_ref[me] = blocks[1, me]
-    for hop in HOPS:
-        send(1, hop)
+    pl.semaphore_wait(known.at[2], 1)
+    for i, offset in LAST:
+        send(i, (offset,))
     for i in range(2):
         zero = jnp.zeros((width, 128), jnp.float32)
         sums = (zero, zero)
@@ -150,6 +175,7 @@
             pltpu.SemaphoreType.DMA((2, NZ)),
             pltpu.SemaphoreType.DMA((2,)),
             pltpu.SemaphoreType.DMA((2, NZ)),
+            pltpu.SemaphoreType.REGULAR((3,)),
         ],
         compiler_params=pltpu.CompilerParams(
             collective_id=0, has_side_effects=True, vmem_limit_bytes=58 << 20

time: 109 us -> 106 us (0.972)
  Pallas kernels: 108 us -> 105 us
    pallas_call x1, Pallas kernels: 106 us -> 103 us  [shards(): pl.pallas_call(move_kernel, out_shape=(pltpu.VMEM(block, jnp.float32), pl...]
where the time goes in v2:
time: 106 us; the launch traced here: 105 us
  Pallas kernels  105 us (99%)
    pallas_call x1, Pallas kernels, shards(): pl.pallas_call(move_kernel, out_shape=(pltpu.VMEM(block, jnp.float32), pl...  103 us
    pallas_call x1, Pallas kernels, shards(): pl.pallas_call(scale_kernel, out_shape=(wide, wide), in_specs=[pl.BlockSp...  2.16 us

profile of v2, /device:TPU:1, one launch (start us, length us, event | category | flops | bytes accessed | tf_op | source)
XLA Modules:
  0.0 105.4 jit_solution(8157837756093879696)
XLA Ops:
  0.6 102.6 %move.1 = (f32[64,32,256]{2,1,0:T(8,128)S(1)}, f32[64,32,256]{2,1,0:T(8,128)S(1)}, f32[4,32,128]{2,1,0:T(8,128)S(1)}) custom-call(f32[256,2048]{1,0:T(8,128)} %a_ref.1, f32[256,2048]{1,0:T(8,128)} %b_ref.1), custom_call_target="tpu_custom_call" | custom-call | tf_op jit(solution)/shard_map/move/pallas_call | solution.py:163
  103.2 2.2 %scale.1 = (f32[32,16384]{1,0:T(8,128)}, f32[32,16384]{1,0:T(8,128)}) custom-call(f32[64,32,256]{2,1,0:T(8,128)S(1)} %get-tuple-element.7.ra_ref, f32[64,32,256]{2,1,0:T(8,128)S(1)} %get-tuple-element.8.rb_ref, f32[4,32,128]{2,1,0:T(8,128)S(1)} %get-tuple-element.9.stats_ref), custom_call_target="tpu_custom_call" | custom-call | tf_op jit(solution)/shard_map/scale/pallas_call | solution.py:186

commit v3 on v2

--- a/solution.py
+++ b/solution.py
@@ -12,20 +12,18 @@
 PLANE = NY * NC
 PEERS = NZ * PLANE
 HOPS = (1, 7, 2, 6, 3, 5, 4, 0)
-OFFSETS = tuple(
-    ((5 * k + 5) % NZ, (k // NZ * 3 + k) % NY, k // (NZ * NY)) for k in range(PEERS)
+NEAR = tuple((0, k // NC, k % NC) for k in range(1, PLANE)) + tuple(
+    (hop, 0, dc) for hop in (1, 7) for dc in range(NC)
 )
-NEAR = tuple(
-    (hop, dy, dc)
-    for hop, dy, dc in OFFSETS
-    if (hop == 0 and dy + dc > 0) or (hop in (1, 7) and dy == 0)
+FIRST = tuple((hop, 0, dc) for dc in range(NC) for hop in (1, 7))
+SECOND = tuple((hop, 0, dc) for dc in range(NC) for hop in (2, 6))
+SHIFTS = ((0, 0), (4, 2), (3, 3), (5, 1), (2, 0), (6, 2), (1, 1), (7, 3))
+ROUNDS = tuple(
+    (hop, (turn + shift) % NY, (turn + shift) // NY % NC)
+    for turn in range(PLANE)
+    for hop, shift in SHIFTS
 )
-FIRST = ((1, 0, 0), (7, 0, 0), (1, 0, 1), (7, 0, 1))
-SECOND = tuple((hop, dy, dc) for dy in (1, 2, 3) for dc in (0, 1) for hop in (1, 7))
-THIRD = tuple(o for o in OFFSETS if o[0] not in (1, 7, 4) and o != (0, 0, 0))
-LAST = tuple((0, o) for o in OFFSETS if o[0] == 4) + tuple(
-    (1, o) for o in OFFSETS if o != (0, 0, 0)
-)
+REST = tuple(o for o in ROUNDS if o not in FIRST + SECOND + ((0, 0, 0),))
 
 
 def move_kernel(
@@ -41,7 +39,8 @@
     sources, landed = (a_ref, b_ref), (ra_ref, rb_ref)
 
     def peer(hop, dy, dc):
-        return lax.rem(z + hop, NZ) * PLANE + lax.rem(y + dy, NY) * NC + lax.rem(c + dc, NC)
+        across = dy + c * (NY - 2 * dy)
+        return lax.rem(z + hop, NZ) * PLANE + lax.rem(y + across, NY) * NC + lax.rem(c + dc, NC)
 
     def signal(semaphore, *offset):
         pl.semaphore_signal(
@@ -94,8 +93,8 @@
     barrier = pltpu.get_barrier_semaphore()
     for offset in NEAR:
         signal(barrier, *offset)
-    for i in range(2):
-        for hop in HOPS:
+    for hop in HOPS:
+        for i in range(2):
             load(i, hop).start()
     turn(0, 1)
     turn(0, 7)
@@ -103,24 +102,27 @@
     signal(known.at[0], 1, 0, 0)
     signal(known.at[0], 7, 0, 0)
     send(0, FIRST)
-    turn(0, 2)
-    turn(0, 6)
+    turn(1, 1)
+    turn(1, 7)
+    for i in range(2):
+        turn(i, 2)
+        turn(i, 6)
+    send(1, FIRST)
     pl.semaphore_wait(known.at[0], 2)
     signal(known.at[1], 2, 0, 0)
     signal(known.at[1], 6, 0, 0)
     send(0, SECOND)
-    for hop in (3, 5, 4, 0):
-        turn(0, hop)
+    send(1, SECOND)
+    for i in range(2):
+        for hop in (3, 5, 4, 0):
+            turn(i, hop)
     pl.semaphore_wait(known.at[1], 2)
     signal(known.at[2], 7, 0, 0)
-    send(0, THIRD)
-    for hop in HOPS:
-        turn(1, hop)
     ra_ref[me] = blocks[0, me]
     rb_ref[me] = blocks[1, me]
     pl.semaphore_wait(known.at[2], 1)
-    for i, offset in LAST:
-        send(i, (offset,))
+    send(0, REST)
+    send(1, REST)
     for i in range(2):
         zero = jnp.zeros((width, 128), jnp.float32)
         sums = (zero, zero)

time: 106 us -> 104 us (0.981)
    pallas_call x1, Pallas kernels: 103 us -> 101 us  [shards(): pl.pallas_call(move_kernel, out_shape=(pltpu.VMEM(block, jnp.float32), pl...]
where the time goes in v3:
time: 104 us
  Pallas kernels  104 us (100%)
    pallas_call x1, Pallas kernels, shards(): pl.pallas_call(move_kernel, out_shape=(pltpu.VMEM(block, jnp.float32), pl...  101 us
    pallas_call x1, Pallas kernels, shards(): pl.pallas_call(scale_kernel, out_shape=(wide, wide), in_specs=[pl.BlockSp...  2.16 us

profile of v3, /device:TPU:1, one launch (start us, length us, event | category | flops | bytes accessed | tf_op | source)
XLA Modules:
  0.0 104.1 jit_solution(10656320001855312829)
XLA Ops:
  0.6 101.3 %move.1 = (f32[64,32,256]{2,1,0:T(8,128)S(1)}, f32[64,32,256]{2,1,0:T(8,128)S(1)}, f32[4,32,128]{2,1,0:T(8,128)S(1)}) custom-call(f32[256,2048]{1,0:T(8,128)} %a_ref.1, f32[256,2048]{1,0:T(8,128)} %b_ref.1), custom_call_target="tpu_custom_call" | custom-call | tf_op jit(solution)/shard_map/move/pallas_call | solution.py:165
  102.0 2.2 %scale.1 = (f32[32,16384]{1,0:T(8,128)}, f32[32,16384]{1,0:T(8,128)}) custom-call(f32[64,32,256]{2,1,0:T(8,128)S(1)} %get-tuple-element.7.ra_ref, f32[64,32,256]{2,1,0:T(8,128)S(1)} %get-tuple-element.8.rb_ref, f32[4,32,128]{2,1,0:T(8,128)S(1)} %get-tuple-element.9.stats_ref), custom_call_target="tpu_custom_call" | custom-call | tf_op jit(solution)/shard_map/scale/pallas_call | solution.py:188

commit v4 on v3

--- a/solution.py
+++ b/solution.py
@@ -12,9 +12,7 @@
 PLANE = NY * NC
 PEERS = NZ * PLANE
 HOPS = (1, 7, 2, 6, 3, 5, 4, 0)
-NEAR = tuple((0, k // NC, k % NC) for k in range(1, PLANE)) + tuple(
-    (hop, 0, dc) for hop in (1, 7) for dc in range(NC)
-)
+LINE = ((0, 0, 1),) + tuple((hop, 0, dc) for hop in (1, 7) for dc in range(NC))
 FIRST = tuple((hop, 0, dc) for dc in range(NC) for hop in (1, 7))
 SECOND = tuple((hop, 0, dc) for dc in range(NC) for hop in (2, 6))
 SHIFTS = ((0, 0), (4, 2), (3, 3), (5, 1), (2, 0), (6, 2), (1, 1), (7, 3))
@@ -24,6 +22,13 @@
     for hop, shift in SHIFTS
 )
 REST = tuple(o for o in ROUNDS if o not in FIRST + SECOND + ((0, 0, 0),))
+FINAL = ((1, 1), (3, 1))
+FAR = tuple(o for o in REST if o[0] == 4)
+BODY = tuple(o for o in REST if o[0] != 4 and o[1:] not in FINAL)
+STEP = len(BODY) // len(FAR) - 1
+SPREAD = tuple(
+    o for k in range(len(FAR)) for o in (FAR[k],) + BODY[k * STEP : (k + 1) * STEP]
+) + BODY[len(FAR) * STEP :]
 
 
 def move_kernel(
@@ -47,6 +52,10 @@
             semaphore, inc=1, device_id=(peer(*offset), group), device_id_type=MESH
         )
 
+    def greet(semaphore, k):
+        to = z * PLANE + lax.rem(y + k + NY, NY) * NC + c
+        pl.semaphore_signal(semaphore, inc=1, device_id=(to, group), device_id_type=MESH)
+
     def load(i, hop):
         plane = lax.rem(z + hop, NZ)
         columns = pl.ds(pl.multiple_of(plane * span, span), span)
@@ -67,6 +76,7 @@
 
     def send(i, offsets):
         for hop, dy, dc in offsets:
+            hop = lax.rem(hop + NZ, NZ)
             to = peer(hop, dy, dc)
             pltpu.make_async_remote_copy(
                 src_ref=blocks.at[i, to],
@@ -91,16 +101,23 @@
         return low, high
 
     barrier = pltpu.get_barrier_semaphore()
-    for offset in NEAR:
+    for hop in (1, 7):
+        load(0, hop).start()
+    for offset in LINE:
         signal(barrier, *offset)
+    for k in range(1, NY):
+        pl.when(y + k < NY)(functools.partial(greet, barrier, k))
+    turn(0, 1)
+    turn(0, 7)
     for hop in HOPS:
         for i in range(2):
-            load(i, hop).start()
-    turn(0, 1)
-    turn(0, 7)
-    pl.semaphore_wait(barrier, len(NEAR))
+            if i > 0 or hop not in (1, 7):
+                load(i, hop).start()
+    pl.semaphore_wait(barrier, len(LINE) + y)
     signal(known.at[0], 1, 0, 0)
     signal(known.at[0], 7, 0, 0)
+    for k in range(1, NY):
+        pl.when(y >= k)(functools.partial(greet, known.at[2], -k))
     send(0, FIRST)
     turn(1, 1)
     turn(1, 7)
@@ -117,12 +134,21 @@
         for hop in (3, 5, 4, 0):
             turn(i, hop)
     pl.semaphore_wait(known.at[1], 2)
-    signal(known.at[2], 7, 0, 0)
+
+    @pl.when(y < NY - 1)
+    def _():
+        pl.semaphore_wait(known.at[2], NY - 1 - y)
+
+    for k in range(1, NY):
+        greet(known.at[3], k)
     ra_ref[me] = blocks[0, me]
     rb_ref[me] = blocks[1, me]
-    pl.semaphore_wait(known.at[2], 1)
+    pl.semaphore_wait(known.at[3], NY - 1)
     send(0, REST)
-    send(1, REST)
+    send(1, SPREAD)
+    for plane in range(NZ):
+        ahead = tuple((plane - z, dy, dc) for dy, dc in FINAL)
+        pl.when(lax.rem(plane - z + NZ, NZ) != 4)(functools.partial(send, 1, ahead))
     for i in range(2):
         zero = jnp.zeros((width, 128), jnp.float32)
         sums = (zero, zero)
@@ -177,7 +203,7 @@
             pltpu.SemaphoreType.DMA((2, NZ)),
             pltpu.SemaphoreType.DMA((2,)),
             pltpu.SemaphoreType.DMA((2, NZ)),
-            pltpu.SemaphoreType.REGULAR((3,)),
+            pltpu.SemaphoreType.REGULAR((4,)),
         ],
         compiler_params=pltpu.CompilerParams(
             collective_id=0, has_side_effects=True, vmem_limit_bytes=58 << 20

time: 104 us -> 103 us (level); the launches traced: 104 us -> 102 us
  Pallas kernels: 104 us -> 101 us
    pallas_call x1, Pallas kernels: 101 us -> 98.9 us  [shards(): pl.pallas_call(move_kernel, out_shape=(pltpu.VMEM(block, jnp.float32), pl...]
where the time goes in v4:
time: 103 us; the launch traced here: 102 us
  Pallas kernels  101 us (98%)
    pallas_call x1, Pallas kernels, shards(): pl.pallas_call(move_kernel, out_shape=(pltpu.VMEM(block, jnp.float32), pl...  98.9 us
    pallas_call x1, Pallas kernels, shards(): pl.pallas_call(scale_kernel, out_shape=(wide, wide), in_specs=[pl.BlockSp...  2.16 us

profile of v4, /device:TPU:1, one launch (start us, length us, event | category | flops | bytes accessed | tf_op | source)
XLA Modules:
  0.0 101.7 jit_solution(8440955107636288684)
XLA Ops:
  0.6 98.9 %move.1 = (f32[64,32,256]{2,1,0:T(8,128)S(1)}, f32[64,32,256]{2,1,0:T(8,128)S(1)}, f32[4,32,128]{2,1,0:T(8,128)S(1)}) custom-call(f32[256,2048]{1,0:T(8,128)} %a_ref.1, f32[256,2048]{1,0:T(8,128)} %b_ref.1), custom_call_target="tpu_custom_call" | custom-call | tf_op jit(solution)/shard_map/move/pallas_call | solution.py:191
  99.6 2.2 %scale.1 = (f32[32,16384]{1,0:T(8,128)}, f32[32,16384]{1,0:T(8,128)}) custom-call(f32[64,32,256]{2,1,0:T(8,128)S(1)} %get-tuple-element.7.ra_ref, f32[64,32,256]{2,1,0:T(8,128)S(1)} %get-tuple-element.8.rb_ref, f32[4,32,128]{2,1,0:T(8,128)S(1)} %get-tuple-element.9.stats_ref), custom_call_target="tpu_custom_call" | custom-call | tf_op jit(solution)/shard_map/scale/pallas_call | solution.py:214

commit v5 on v4

--- a/solution.py
+++ b/solution.py
@@ -25,7 +25,7 @@
 FINAL = ((1, 1), (3, 1))
 FAR = tuple(o for o in REST if o[0] == 4)
 BODY = tuple(o for o in REST if o[0] != 4 and o[1:] not in FINAL)
-STEP = len(BODY) // len(FAR) - 1
+STEP = len(BODY) // len(FAR) // 2
 SPREAD = tuple(
     o for k in range(len(FAR)) for o in (FAR[k],) + BODY[k * STEP : (k + 1) * STEP]
 ) + BODY[len(FAR) * STEP :]

time: 103 us -> 102 us (level); the launches traced: 102 us -> 102 us
  no operation moved by 1% of the time
where the time goes in v5:
time: 102 us
  Pallas kernels  101 us (99%)
    pallas_call x1, Pallas kernels, shards(): pl.pallas_call(move_kernel, out_shape=(pltpu.VMEM(block, jnp.float32), pl...  99.2 us
    pallas_call x1, Pallas kernels, shards(): pl.pallas_call(scale_kernel, out_shape=(wide, wide), in_specs=[pl.BlockSp...  2.16 us

profile of v5, /device:TPU:1, one launch (start us, length us, event | category | flops | bytes accessed | tf_op | source)
XLA Modules:
  0.0 102.0 jit_solution(14155962900661230917)
XLA Ops:
  0.6 99.2 %move.1 = (f32[64,32,256]{2,1,0:T(8,128)S(1)}, f32[64,32,256]{2,1,0:T(8,128)S(1)}, f32[4,32,128]{2,1,0:T(8,128)S(1)}) custom-call(f32[256,2048]{1,0:T(8,128)} %a_ref.1, f32[256,2048]{1,0:T(8,128)} %b_ref.1), custom_call_target="tpu_custom_call" | custom-call | tf_op jit(solution)/shard_map/move/pallas_call | solution.py:191
  99.9 2.2 %scale.1 = (f32[32,16384]{1,0:T(8,128)}, f32[32,16384]{1,0:T(8,128)}) custom-call(f32[64,32,256]{2,1,0:T(8,128)S(1)} %get-tuple-element.7.ra_ref, f32[64,32,256]{2,1,0:T(8,128)S(1)} %get-tuple-element.8.rb_ref, f32[4,32,128]{2,1,0:T(8,128)S(1)} %get-tuple-element.9.stats_ref), custom_call_target="tpu_custom_call" | custom-call | tf_op jit(solution)/shard_map/scale/pallas_call | solution.py:214

commit v6 on v5

--- a/solution.py
+++ b/solution.py
@@ -152,7 +152,7 @@
     for i in range(2):
         zero = jnp.zeros((width, 128), jnp.float32)
         sums = (zero, zero)
-        for hop in HOPS:
+        for hop in (4, 0, 3, 5, 2, 6, 1, 7):
             sums = gather(i, hop, sums)
         low = jnp.sum(sums[0], axis=1, keepdims=True) * (1.0 / total)
         high = jnp.sum(sums[1], axis=1, keepdims=True) * (1.0 / total)

time: 102 us -> 102 us (level)
  no operation moved by 1% of the time
where the time goes in v6:
time: 102 us
  Pallas kernels  101 us (99%)
    pallas_call x1, Pallas kernels, shards(): pl.pallas_call(move_kernel, out_shape=(pltpu.VMEM(block, jnp.float32), pl...  99.3 us
    pallas_call x1, Pallas kernels, shards(): pl.pallas_call(scale_kernel, out_shape=(wide, wide), in_specs=[pl.BlockSp...  2.16 us

profile of v6, /device:TPU:1, one launch (start us, length us, event | category | flops | bytes accessed | tf_op | source)
XLA Modules:
  0.0 102.1 jit_solution(929022011681438770)
XLA Ops:
  0.6 99.3 %move.1 = (f32[64,32,256]{2,1,0:T(8,128)S(1)}, f32[64,32,256]{2,1,0:T(8,128)S(1)}, f32[4,32,128]{2,1,0:T(8,128)S(1)}) custom-call(f32[256,2048]{1,0:T(8,128)} %a_ref.1, f32[256,2048]{1,0:T(8,128)} %b_ref.1), custom_call_target="tpu_custom_call" | custom-call | tf_op jit(solution)/shard_map/move/pallas_call | solution.py:191
  99.9 2.2 %scale.1 = (f32[32,16384]{1,0:T(8,128)}, f32[32,16384]{1,0:T(8,128)}) custom-call(f32[64,32,256]{2,1,0:T(8,128)S(1)} %get-tuple-element.7.ra_ref, f32[64,32,256]{2,1,0:T(8,128)S(1)} %get-tuple-element.8.rb_ref, f32[4,32,128]{2,1,0:T(8,128)S(1)} %get-tuple-element.9.stats_ref), custom_call_target="tpu_custom_call" | custom-call | tf_op jit(solution)/shard_map/scale/pallas_call | solution.py:214
